TPU v7x, 32 devices: a whole 2x2x4 slice. The times are simulated.
32 devices in a mesh: blocks: 2 (over y), gz: 8 (over z, x), gy: 2 (over core).
Axes of the slice: x: 2, y: 2, z: 4, core: 2. Of those that a mesh axis runs over, the one named last changes fastest.
Arguments:
- view_a: float32 [256, 32, 512], P(('blocks', 'gz'), 'gy'), parts along dimension 0, may hold values from 0.5 to 2
- view_b_own: float32 [1024, 32, 128], P(('blocks', 'gz'), 'gy'), parts along dimension 0, may hold values from 0.5 to 2
- spread_a: float32 [3, 31], replicated, may hold values from 0.05 to 1
- spread_b: float32 [3, 31], replicated, may hold values from 0.05 to 1
Outputs:
- estimate: float32 [256, 32, 512], P(('blocks', 'gz'), 'gy'), parts along dimension 0
There are 2 independent parts, one for each index of `blocks`. A program takes and returns all parts, laid end to end along the dimension named above; an argument that names none is the same for every part. Nothing has to cross between parts.
All inputs are finite; a program needn't handle non-finite values.
Results may differ from a plain program's by a relative error of at most 0.0001.
Values sent between devices are 32-bit elements; how exact they have to be, the bound alone decides.
A program may use at most 64 MiB of HBM per device.

v0:
```python
import jax
import jax.numpy as jnp
from jax import lax
from jax.sharding import PartitionSpec as P


def padded(cells, sides, width):
    for axis, dim in sides:
        count = lax.axis_size(axis)
        ends = count - 1
        head = lax.slice_in_dim(cells, 0, width, axis=dim)
        tail = lax.slice_in_dim(cells, cells.shape[dim] - width, cells.shape[dim], axis=dim)
        cells = jnp.concatenate(
            [
                lax.ppermute(tail, axis, [(i, (i + 1) % count) for i in range(ends)]),
                cells,
                lax.ppermute(head, axis, [((i + 1) % count, i) for i in range(ends)]),
            ],
            axis=dim,
        )
    return cells


def band_table(weights, count_in, count_out, offset):
    source = jnp.arange(count_in, dtype=jnp.int32)[:, None]
    target = jnp.arange(count_out, dtype=jnp.int32)[None, :]
    spread = source - target + offset
    table = jnp.zeros((count_in, count_out), jnp.float32)
    for place in range(weights.shape[0]):
        table = table + jnp.where(spread == place, weights[place], jnp.float32(0.0))
    return table


def blur(volume, kernels):
    count_z, count_y, count_x = volume.shape
    radius = (kernels.shape[1] - 1) // 2
    table_x = band_table(kernels[2], count_x, count_x, radius)
    along_x = jnp.einsum("zyx,xw->zyw", volume, table_x, precision=lax.Precision.HIGHEST)
    table_y = band_table(kernels[1], count_y + 2 * radius, count_y, 0)
    widened = padded(along_x, (("gy", 1),), radius)
    narrow_y = jnp.einsum("zyx,yw->zwx", widened, table_y, precision=lax.Precision.HIGHEST)
    along_y = padded(narrow_y, (("gz", 0),), radius)
    table_z = band_table(kernels[0], count_z + 2 * radius, count_z, 0)
    return jnp.einsum("zyx,zw->wyx", along_y, table_z, precision=lax.Precision.HIGHEST)


def shards(view_a, view_b_own, spread_a, spread_b):
    arrived = lax.all_to_all(view_b_own, "gz", split_axis=2, concat_axis=0, tiled=True)
    view_b = jnp.transpose(arrived, (2, 1, 0))[:, :, ::-1]
    blur_a = spread_a / jnp.sum(spread_a, axis=1, keepdims=True)
    blur_b = spread_b / jnp.sum(spread_b, axis=1, keepdims=True)
    estimate = 0.5 * (view_a + view_b)
    for measured, kernels in ((view_a, blur_a), (view_b, blur_b)):
        quotient = measured / blur(estimate, kernels)
        estimate = estimate * blur(quotient, kernels[:, ::-1])
    return estimate


def solution(mesh):
    in_specs = (P(("blocks", "gz"), "gy", None), P(("blocks", "gz"), "gy", None), P(), P())
    out_specs = P(("blocks", "gz"), "gy", None)
    return jax.shard_map(shards, mesh=mesh, in_specs=in_specs, out_specs=out_specs, check_vma=False)
```

profile of v0, /device:TPU:9, one launch (start us, length us, event | category | flops | bytes accessed | tf_op | source)
XLA Modules:
  0.0 425.9 jit_solution(4899203801518568885)
XLA Ops:
  0.0 1.6 copy.22
  1.6 1.4 reshape.758
  3.0 5.7 %all-to-all-start = ((f32[8,1,16384]{2,1,0:T(1,128)}), f32[8,1,16384]{2,1,0:T(1,128)S(1)}, u32[]{:S(2)}, u32[]{:S(2)}) async-start(f32[8,1,16384]{2,1,0:T(1,128)} %reshape.758), calls=%async_computation | async-start | bytes 1048576 | tf_op jit(solution)/shard_map/all_to_all | solution.py:48
  10.4 9.5 %all-to-all-done = f32[8,1,16384]{2,1,0:T(1,128)S(1)} async-done(((f32[8,1,16384]{2,1,0:T(1,128)}), f32[8,1,16384]{2,1,0:T(1,128)S(1)}, u32[]{:S(2)}, u32[]{:S(2)}) %all-to-all-start) | async-done | bytes 524320 | tf_op jit(solution)/shard_map/all_to_all | solution.py:48
  20.3 1.9 reduce
  24.7 25.4 %fusion.122 = f32[16,16,512]{2,1,0:T(8,128)S(1)} fusion(f32[16,16,512]{2,0,1:T(8,128)S(1)} %add_multiply_fusion, f32[]{:T(128)} %bitcast.100, f32[]{:T(128)} %bitcast.99, f32[]{:T(128)} %bitcast.98, f32[]{:T(128)} %bitcast.97, f32[]{:T(128)} %bitcast.96, f32[]{:T(128)} %bitcast.95, f32[]{:T(128)} %bitcast.94, f32[]{:T(128)} %bitcast.93, f32[]{:T(128)} %bitcast.92, ...), kind=kOutput, calls=%fused_computation.114 | convolution fusion | flops 829947904 | bytes 1048700 | tf_op jit(solution)/shard_map/zyx,xw->zyw/dot_general | solution.py:38
  50.2 1.3 collective-permute-start
  51.5 5.4 %collective-permute-start.1 = (f32[16,15,512]{2,1,0:T(8,128)S(1)}, f32[16,15,512]{2,1,0:T(8,128)S(1)}, u32[]{:S(2)}, u32[]{:S(2)}) collective-permute-start(f32[16,15,512]{2,1,0:T(8,128)S(1)} %get-tuple-element.20), channel_id=1, source_target_pairs={{1,0},{3,2},{5,4},{7,6},{9,8},{11,10},{13,12},{15,14},{17,16},{19,... | collective-permute-start | bytes 1474568 | tf_op jit(solution)/shard_map/ppermute | solution.py:17
  57.6 0.7 fusion.2089
  58.3 20.3 %fusion.53 = f32[16,16,512]{2,1,0:T(8,128)S(1)} fusion(f32[16,15,512]{2,1,0:T(8,128)S(1)} %collective-permute-done.1, f32[16,16,512]{2,1,0:T(8,128)S(1)} %fusion.122, f32[16,15,512]{2,1,0:T(8,128)S(1)} %collective-permute-done, f32[]{:T(128)} %bitcast.66, f32[]{:T(128)} %bitcast.65, f32[]{:T(128)} %bitcast.64, f32[]{:T(128)} %bitcast.63, f32[]{:T(128)} %bitcast.62, ...), kind=kOutput, calls=%fused_computation.47 | convolution fusion | flops 73173856 | bytes 2031740 | tf_op jit(solution)/shard_map/zyx,yw->zwx/dot_general | solution.py:41
  78.8 1.9 collective-permute-start.2
  80.7 4.4 %collective-permute-start.3 = (f32[15,16,512]{2,1,0:T(8,128)S(1)}, f32[15,16,512]{2,1,0:T(8,128)S(1)}, u32[]{:S(2)}, u32[]{:S(2)}) collective-permute-start(f32[15,16,512]{2,1,0:T(8,128)S(1)} %get-tuple-element.18), channel_id=1, source_target_pairs={{2,0},{4,2},{6,4},{8,6},{10,8},{12,10},{14,12},{3,1},{5,3},{7,5},{... | collective-permute-start | bytes 1474568 | tf_op jit(solution)/shard_map/ppermute | solution.py:17
  85.9 15.8 %collective-permute-done.2 = f32[15,16,512]{2,1,0:T(8,128)S(1)} collective-permute-done((f32[15,16,512]{2,1,0:T(8,128)S(1)}, f32[15,16,512]{2,1,0:T(8,128)S(1)}, u32[]{:S(2)}, u32[]{:S(2)}) %collective-permute-start.2) | collective-permute-done | bytes 491552 | tf_op jit(solution)/shard_map/ppermute | solution.py:15
  101.6 3.6 collective-permute-done.3
  105.4 21.1 %fusion.32 = f32[16,16,512]{2,0,1:T(8,128)S(1)} fusion(f32[46,16,512]{2,1,0:T(8,128)S(1)} %pad_maximum_fusion, f32[16,16,512]{2,1,0:T(8,128)S(1)} %copy-done, f32[]{:T(128)} %bitcast.34, f32[]{:T(128)} %bitcast.33, f32[]{:T(128)} %bitcast.32, f32[]{:T(128)} %bitcast.31, f32[]{:T(128)} %bitcast.30, f32[]{:T(128)} %bitcast.29, f32[]{:T(128)} %bitcast.28, ...), kind=kOutput, calls=%fused_computation.40 | convolution fusion | flops 72551264 | bytes 2556028 | tf_op jit(solution)/shard_map/zyx,zw->wyx/dot_general | solution.py:44
  126.5 25.4 %fusion.120 = f32[16,16,512]{2,1,0:T(8,128)S(1)} fusion(f32[16,16,512]{2,0,1:T(8,128)S(1)} %fusion.32, f32[]{:T(128)} %bitcast.100, f32[]{:T(128)} %bitcast.99, f32[]{:T(128)} %bitcast.98, f32[]{:T(128)} %bitcast.97, f32[]{:T(128)} %bitcast.96, f32[]{:T(128)} %bitcast.95, f32[]{:T(128)} %bitcast.94, f32[]{:T(128)} %bitcast.93, f32[]{:T(128)} %bitcast.92, ...), kind=kOutput, calls=%fused_computation.112 | convolution fusion | flops 829947904 | bytes 1048700 | tf_op jit(solution)/shard_map/zyx,xw->zyw/dot_general | solution.py:38
  152.1 1.3 collective-permute-start.4
  153.4 3.1 collective-permute-start.5
  156.5 1.5 collective-permute-done.5
  157.9 20.3 %fusion.50 = f32[16,16,512]{2,1,0:T(8,128)S(1)} fusion(f32[16,15,512]{2,1,0:T(8,128)S(1)} %collective-permute-done.5, f32[16,16,512]{2,1,0:T(8,128)S(1)} %fusion.120, f32[16,15,512]{2,1,0:T(8,128)S(1)} %collective-permute-done.4, f32[]{:T(128)} %bitcast.66, f32[]{:T(128)} %bitcast.65, f32[]{:T(128)} %bitcast.64, f32[]{:T(128)} %bitcast.63, f32[]{:T(128)} %bitcast.62, ...), kind=kOutput, calls=%fused_computation.46 | convolution fusion | flops 73173856 | bytes 2031740 | tf_op jit(solution)/shard_map/zyx,yw->zwx/dot_general | solution.py:41
  178.4 1.9 collective-permute-start.6
  180.3 4.5 %collective-permute-start.7 = (f32[15,16,512]{2,1,0:T(8,128)S(1)}, f32[15,16,512]{2,1,0:T(8,128)S(1)}, u32[]{:S(2)}, u32[]{:S(2)}) collective-permute-start(f32[15,16,512]{2,1,0:T(8,128)S(1)} %get-tuple-element.14), channel_id=1, source_target_pairs={{2,0},{4,2},{6,4},{8,6},{10,8},{12,10},{14,12},{3,1},{5,3},{7,5},{... | collective-permute-start | bytes 1474568 | tf_op jit(solution)/shard_map/ppermute | solution.py:17
  185.0 0.7 fusion.2083
  186.4 14.9 %collective-permute-done.6 = f32[15,16,512]{2,1,0:T(8,128)S(1)} collective-permute-done((f32[15,16,512]{2,1,0:T(8,128)S(1)}, f32[15,16,512]{2,1,0:T(8,128)S(1)}, u32[]{:S(2)}, u32[]{:S(2)}) %collective-permute-start.6) | collective-permute-done | bytes 491552 | tf_op jit(solution)/shard_map/ppermute | solution.py:15
  201.3 3.6 collective-permute-done.7
  205.0 20.9 %fusion.35 = f32[16,16,512]{2,0,1:T(8,128)S(1)} fusion(f32[16,16,512]{2,0,1:T(8,128)S(1)} %add_multiply_fusion, f32[46,16,512]{2,1,0:T(8,128)S(1)} %pad_maximum_fusion.1, f32[]{:T(128)} %bitcast.34, f32[]{:T(128)} %bitcast.33, f32[]{:T(128)} %bitcast.32, f32[]{:T(128)} %bitcast.31, f32[]{:T(128)} %bitcast.30, f32[]{:T(128)} %bitcast.29, f32[]{:T(128)} %bitcast.28, ...), kind=kOutput, calls=%fused_computation.41 | convolution fusion | flops 72551264 | bytes 2556028 | tf_op jit(solution)/shard_map/zyx,zw->wyx/dot_general | solution.py:44
  225.9 25.4 %fusion.118 = f32[16,16,512]{2,1,0:T(8,128)S(1)} fusion(f32[16,16,512]{2,0,1:T(8,128)S(1)} %fusion.35, f32[]{:T(128)} %bitcast.201, f32[]{:T(128)} %bitcast.200, f32[]{:T(128)} %bitcast.199, f32[]{:T(128)} %bitcast.198, f32[]{:T(128)} %bitcast.197, f32[]{:T(128)} %bitcast.196, f32[]{:T(128)} %bitcast.195, f32[]{:T(128)} %bitcast.194, f32[]{:T(128)} %bitcast.193, ...), kind=kOutput, calls=%fused_computation.110 | convolution fusion | flops 829947904 | bytes 1048700 | tf_op jit(solution)/shard_map/zyx,xw->zyw/dot_general | solution.py:38
  251.4 1.3 collective-permute-start.8
  252.7 3.1 collective-permute-start.9
  256.5 0.7 fusion.2084
  257.3 20.4 %fusion.47 = f32[16,16,512]{2,1,0:T(8,128)S(1)} fusion(f32[16,15,512]{2,1,0:T(8,128)S(1)} %collective-permute-done.9, f32[16,16,512]{2,1,0:T(8,128)S(1)} %fusion.118, f32[16,15,512]{2,1,0:T(8,128)S(1)} %collective-permute-done.8, f32[]{:T(128)} %bitcast.167, f32[]{:T(128)} %bitcast.166, f32[]{:T(128)} %bitcast.165, f32[]{:T(128)} %bitcast.164, ...), kind=kOutput, calls=%fused_computation.45 | convolution fusion | flops 73173856 | bytes 2031740 | tf_op jit(solution)/shard_map/zyx,yw->zwx/dot_general | solution.py:41
  277.7 1.9 collective-permute-start.10
  279.7 4.5 %collective-permute-start.11 = (f32[15,16,512]{2,1,0:T(8,128)S(1)}, f32[15,16,512]{2,1,0:T(8,128)S(1)}, u32[]{:S(2)}, u32[]{:S(2)}) collective-permute-start(f32[15,16,512]{2,1,0:T(8,128)S(1)} %get-tuple-element.10), channel_id=1, source_target_pairs={{2,0},{4,2},{6,4},{8,6},{10,8},{12,10},{14,12},{3,1},{5,3},{7,5},{... | collective-permute-start | bytes 1474568 | tf_op jit(solution)/shard_map/ppermute | solution.py:17
  284.2 0.7 fusion.2086
  284.9 15.7 %collective-permute-done.10 = f32[15,16,512]{2,1,0:T(8,128)S(1)} collective-permute-done((f32[15,16,512]{2,1,0:T(8,128)S(1)}, f32[15,16,512]{2,1,0:T(8,128)S(1)}, u32[]{:S(2)}, u32[]{:S(2)}) %collective-permute-start.10) | collective-permute-done | bytes 491552 | tf_op jit(solution)/shard_map/ppermute | solution.py:15
  300.7 3.6 collective-permute-done.11
  304.4 21.0 %fusion.38 = f32[16,16,512]{2,0,1:T(8,128)S(1)} fusion(f32[16,16,512]{2,0,1:T(8,128)S(1)} %rev.2, f32[46,16,512]{2,1,0:T(8,128)S(1)} %pad_maximum_fusion.2, f32[]{:T(128)} %bitcast.135, f32[]{:T(128)} %bitcast.134, f32[]{:T(128)} %bitcast.133, f32[]{:T(128)} %bitcast.132, f32[]{:T(128)} %bitcast.131, f32[]{:T(128)} %bitcast.130, f32[]{:T(128)} %bitcast.129, ...), kind=kOutput, calls=%fused_computation.42 | convolution fusion | flops 72551264 | bytes 2556028 | tf_op jit(solution)/shard_map/zyx,zw->wyx/dot_general | solution.py:44
  325.4 25.3 %fusion.116 = f32[16,16,512]{2,1,0:T(8,128)S(1)} fusion(f32[16,16,512]{2,0,1:T(8,128)S(1)} %fusion.38, f32[]{:T(128)} %bitcast.201, f32[]{:T(128)} %bitcast.200, f32[]{:T(128)} %bitcast.199, f32[]{:T(128)} %bitcast.198, f32[]{:T(128)} %bitcast.197, f32[]{:T(128)} %bitcast.196, f32[]{:T(128)} %bitcast.195, f32[]{:T(128)} %bitcast.194, f32[]{:T(128)} %bitcast.193, ...), kind=kOutput, calls=%fused_computation.108 | convolution fusion | flops 829947904 | bytes 1048700 | tf_op jit(solution)/shard_map/zyx,xw->zyw/dot_general | solution.py:38
  350.8 1.3 collective-permute-start.12
  352.1 3.1 collective-permute-start.13
  355.2 1.5 collective-permute-done.13
  356.7 20.4 %fusion.44 = f32[16,16,512]{2,1,0:T(8,128)S(1)} fusion(f32[16,15,512]{2,1,0:T(8,128)S(1)} %collective-permute-done.13, f32[16,16,512]{2,1,0:T(8,128)S(1)} %fusion.116, f32[16,15,512]{2,1,0:T(8,128)S(1)} %collective-permute-done.12, f32[]{:T(128)} %bitcast.167, f32[]{:T(128)} %bitcast.166, f32[]{:T(128)} %bitcast.165, f32[]{:T(128)} %bitcast.164, ...), kind=kOutput, calls=%fused_computation.44 | convolution fusion | flops 73173856 | bytes 2031740 | tf_op jit(solution)/shard_map/zyx,yw->zwx/dot_general | solution.py:41
  377.2 1.9 collective-permute-start.14
  379.1 4.3 %collective-permute-start.15 = (f32[15,16,512]{2,1,0:T(8,128)S(1)}, f32[15,16,512]{2,1,0:T(8,128)S(1)}, u32[]{:S(2)}, u32[]{:S(2)}) collective-permute-start(f32[15,16,512]{2,1,0:T(8,128)S(1)} %get-tuple-element.6), channel_id=1, source_target_pairs={{2,0},{4,2},{6,4},{8,6},{10,8},{12,10},{14,12},{3,1},{5,3},{7,5},{... | collective-permute-start | bytes 1474568 | tf_op jit(solution)/shard_map/ppermute | solution.py:17
  383.4 16.7 %collective-permute-done.14 = f32[15,16,512]{2,1,0:T(8,128)S(1)} collective-permute-done((f32[15,16,512]{2,1,0:T(8,128)S(1)}, f32[15,16,512]{2,1,0:T(8,128)S(1)}, u32[]{:S(2)}, u32[]{:S(2)}) %collective-permute-start.14) | collective-permute-done | bytes 491552 | tf_op jit(solution)/shard_map/ppermute | solution.py:15
  400.1 3.6 collective-permute-done.15
  403.9 21.0 %fusion.41 = f32[16,16,512]{2,0,1:T(8,128)S(1)} fusion(f32[16,16,512]{2,0,1:T(8,128)S(1)} %fusion.35, f32[46,16,512]{2,1,0:T(8,128)S(1)} %pad_maximum_fusion.3, f32[]{:T(128)} %bitcast.135, f32[]{:T(128)} %bitcast.134, f32[]{:T(128)} %bitcast.133, f32[]{:T(128)} %bitcast.132, f32[]{:T(128)} %bitcast.131, f32[]{:T(128)} %bitcast.130, f32[]{:T(128)} %bitcast.129, ...), kind=kOutput, calls=%fused_computation.43 | convolution fusion | flops 72551264 | bytes 2556028 | tf_op jit(solution)/shard_map/zyx,zw->wyx/dot_general | solution.py:44
  424.8 1.1 copy.35
  (40 shorter events, 9.2 us)
Async XLA Ops:
  1.6 7.2 %copy-start.1 = (f32[3,31]{1,0:T(4,128)S(1)}, f32[3,31]{1,0:T(4,128)}, u32[]{:S(2)}) copy-start(f32[3,31]{1,0:T(4,128)} %param.6) | copy-start | bytes 1120
  3.0 16.8 %all-to-all-start = ((f32[8,1,16384]{2,1,0:T(1,128)}), f32[8,1,16384]{2,1,0:T(1,128)S(1)}, u32[]{:S(2)}, u32[]{:S(2)}) async-start(f32[8,1,16384]{2,1,0:T(1,128)} %reshape.758), calls=%async_computation | async-start | bytes 1048576 | tf_op jit(solution)/shard_map/all_to_all | solution.py:48
  23.3 1.0 copy-start
  50.2 8.1 %collective-permute-start = (f32[16,15,512]{2,1,0:T(8,128)S(1)}, f32[16,15,512]{2,1,0:T(8,128)S(1)}, u32[]{:S(2)}, u32[]{:S(2)}) collective-permute-start(f32[16,15,512]{2,1,0:T(8,128)S(1)} %get-tuple-element.19), channel_id=1, source_target_pairs={{0,1},{2,3},{4,5},{6,7},{8,9},{10,11},{12,13},{14,15},{16,17},{18,... | collective-permute-start | bytes 1474568 | tf_op jit(solution)/shard_map/ppermute | solution.py:15
  51.5 6.8 %collective-permute-start.1 = (f32[16,15,512]{2,1,0:T(8,128)S(1)}, f32[16,15,512]{2,1,0:T(8,128)S(1)}, u32[]{:S(2)}, u32[]{:S(2)}) collective-permute-start(f32[16,15,512]{2,1,0:T(8,128)S(1)} %get-tuple-element.20), channel_id=1, source_target_pairs={{1,0},{3,2},{5,4},{7,6},{9,8},{11,10},{13,12},{15,14},{17,16},{19,... | collective-permute-start | bytes 1474568 | tf_op jit(solution)/shard_map/ppermute | solution.py:17
  78.8 22.9 %collective-permute-start.2 = (f32[15,16,512]{2,1,0:T(8,128)S(1)}, f32[15,16,512]{2,1,0:T(8,128)S(1)}, u32[]{:S(2)}, u32[]{:S(2)}) collective-permute-start(f32[15,16,512]{2,1,0:T(8,128)S(1)} %get-tuple-element.17), channel_id=1, source_target_pairs={{0,2},{2,4},{4,6},{6,8},{8,10},{10,12},{12,14},{1,3},{3,5},{5,7},{... | collective-permute-start | bytes 1474568 | tf_op jit(solution)/shard_map/ppermute | solution.py:15
  80.7 24.6 %collective-permute-start.3 = (f32[15,16,512]{2,1,0:T(8,128)S(1)}, f32[15,16,512]{2,1,0:T(8,128)S(1)}, u32[]{:S(2)}, u32[]{:S(2)}) collective-permute-start(f32[15,16,512]{2,1,0:T(8,128)S(1)} %get-tuple-element.18), channel_id=1, source_target_pairs={{2,0},{4,2},{6,4},{8,6},{10,8},{12,10},{14,12},{3,1},{5,3},{7,5},{... | collective-permute-start | bytes 1474568 | tf_op jit(solution)/shard_map/ppermute | solution.py:17
  152.1 4.4 %collective-permute-start.4 = (f32[16,15,512]{2,1,0:T(8,128)S(1)}, f32[16,15,512]{2,1,0:T(8,128)S(1)}, u32[]{:S(2)}, u32[]{:S(2)}) collective-permute-start(f32[16,15,512]{2,1,0:T(8,128)S(1)} %get-tuple-element.15), channel_id=1, source_target_pairs={{0,1},{2,3},{4,5},{6,7},{8,9},{10,11},{12,13},{14,15},{16,17},{18,... | collective-permute-start | bytes 1474568 | tf_op jit(solution)/shard_map/ppermute | solution.py:15
  153.4 4.6 %collective-permute-start.5 = (f32[16,15,512]{2,1,0:T(8,128)S(1)}, f32[16,15,512]{2,1,0:T(8,128)S(1)}, u32[]{:S(2)}, u32[]{:S(2)}) collective-permute-start(f32[16,15,512]{2,1,0:T(8,128)S(1)} %get-tuple-element.16), channel_id=1, source_target_pairs={{1,0},{3,2},{5,4},{7,6},{9,8},{11,10},{13,12},{15,14},{17,16},{19,... | collective-permute-start | bytes 1474568 | tf_op jit(solution)/shard_map/ppermute | solution.py:17
  178.2 6.6 %copy-start.2 = (f32[3,31]{1,0:T(4,128)S(1)}, f32[3,31]{1,0:T(4,128)}, u32[]{:S(2)}) copy-start(f32[3,31]{1,0:T(4,128)} %param.7) | copy-start | bytes 1120
  178.4 22.9 %collective-permute-start.6 = (f32[15,16,512]{2,1,0:T(8,128)S(1)}, f32[15,16,512]{2,1,0:T(8,128)S(1)}, u32[]{:S(2)}, u32[]{:S(2)}) collective-permute-start(f32[15,16,512]{2,1,0:T(8,128)S(1)} %get-tuple-element.13), channel_id=1, source_target_pairs={{0,2},{2,4},{4,6},{6,8},{8,10},{10,12},{12,14},{1,3},{3,5},{5,7},{... | collective-permute-start | bytes 1474568 | tf_op jit(solution)/shard_map/ppermute | solution.py:15
  180.3 24.6 %collective-permute-start.7 = (f32[15,16,512]{2,1,0:T(8,128)S(1)}, f32[15,16,512]{2,1,0:T(8,128)S(1)}, u32[]{:S(2)}, u32[]{:S(2)}) collective-permute-start(f32[15,16,512]{2,1,0:T(8,128)S(1)} %get-tuple-element.14), channel_id=1, source_target_pairs={{2,0},{4,2},{6,4},{8,6},{10,8},{12,10},{14,12},{3,1},{5,3},{7,5},{... | collective-permute-start | bytes 1474568 | tf_op jit(solution)/shard_map/ppermute | solution.py:17
  251.4 5.9 %collective-permute-start.8 = (f32[16,15,512]{2,1,0:T(8,128)S(1)}, f32[16,15,512]{2,1,0:T(8,128)S(1)}, u32[]{:S(2)}, u32[]{:S(2)}) collective-permute-start(f32[16,15,512]{2,1,0:T(8,128)S(1)} %get-tuple-element.11), channel_id=1, source_target_pairs={{0,1},{2,3},{4,5},{6,7},{8,9},{10,11},{12,13},{14,15},{16,17},{18,... | collective-permute-start | bytes 1474568 | tf_op jit(solution)/shard_map/ppermute | solution.py:15
  252.7 4.6 %collective-permute-start.9 = (f32[16,15,512]{2,1,0:T(8,128)S(1)}, f32[16,15,512]{2,1,0:T(8,128)S(1)}, u32[]{:S(2)}, u32[]{:S(2)}) collective-permute-start(f32[16,15,512]{2,1,0:T(8,128)S(1)} %get-tuple-element.12), channel_id=1, source_target_pairs={{1,0},{3,2},{5,4},{7,6},{9,8},{11,10},{13,12},{15,14},{17,16},{19,... | collective-permute-start | bytes 1474568 | tf_op jit(solution)/shard_map/ppermute | solution.py:17
  277.7 22.9 %collective-permute-start.10 = (f32[15,16,512]{2,1,0:T(8,128)S(1)}, f32[15,16,512]{2,1,0:T(8,128)S(1)}, u32[]{:S(2)}, u32[]{:S(2)}) collective-permute-start(f32[15,16,512]{2,1,0:T(8,128)S(1)} %get-tuple-element.9), channel_id=1, source_target_pairs={{0,2},{2,4},{4,6},{6,8},{8,10},{10,12},{12,14},{1,3},{3,5},{5,7},{... | collective-permute-start | bytes 1474568 | tf_op jit(solution)/shard_map/ppermute | solution.py:15
  279.7 24.6 %collective-permute-start.11 = (f32[15,16,512]{2,1,0:T(8,128)S(1)}, f32[15,16,512]{2,1,0:T(8,128)S(1)}, u32[]{:S(2)}, u32[]{:S(2)}) collective-permute-start(f32[15,16,512]{2,1,0:T(8,128)S(1)} %get-tuple-element.10), channel_id=1, source_target_pairs={{2,0},{4,2},{6,4},{8,6},{10,8},{12,10},{14,12},{3,1},{5,3},{7,5},{... | collective-permute-start | bytes 1474568 | tf_op jit(solution)/shard_map/ppermute | solution.py:17
  350.8 4.4 %collective-permute-start.12 = (f32[16,15,512]{2,1,0:T(8,128)S(1)}, f32[16,15,512]{2,1,0:T(8,128)S(1)}, u32[]{:S(2)}, u32[]{:S(2)}) collective-permute-start(f32[16,15,512]{2,1,0:T(8,128)S(1)} %get-tuple-element.7), channel_id=1, source_target_pairs={{0,1},{2,3},{4,5},{6,7},{8,9},{10,11},{12,13},{14,15},{16,17},{18,... | collective-permute-start | bytes 1474568 | tf_op jit(solution)/shard_map/ppermute | solution.py:15
  352.1 4.6 %collective-permute-start.13 = (f32[16,15,512]{2,1,0:T(8,128)S(1)}, f32[16,15,512]{2,1,0:T(8,128)S(1)}, u32[]{:S(2)}, u32[]{:S(2)}) collective-permute-start(f32[16,15,512]{2,1,0:T(8,128)S(1)} %get-tuple-element.8), channel_id=1, source_target_pairs={{1,0},{3,2},{5,4},{7,6},{9,8},{11,10},{13,12},{15,14},{17,16},{19,... | collective-permute-start | bytes 1474568 | tf_op jit(solution)/shard_map/ppermute | solution.py:17
  377.2 22.9 %collective-permute-start.14 = (f32[15,16,512]{2,1,0:T(8,128)S(1)}, f32[15,16,512]{2,1,0:T(8,128)S(1)}, u32[]{:S(2)}, u32[]{:S(2)}) collective-permute-start(f32[15,16,512]{2,1,0:T(8,128)S(1)} %get-tuple-element.5), channel_id=1, source_target_pairs={{0,2},{2,4},{4,6},{6,8},{8,10},{10,12},{12,14},{1,3},{3,5},{5,7},{... | collective-permute-start | bytes 1474568 | tf_op jit(solution)/shard_map/ppermute | solution.py:15
  379.1 24.6 %collective-permute-start.15 = (f32[15,16,512]{2,1,0:T(8,128)S(1)}, f32[15,16,512]{2,1,0:T(8,128)S(1)}, u32[]{:S(2)}, u32[]{:S(2)}) collective-permute-start(f32[15,16,512]{2,1,0:T(8,128)S(1)} %get-tuple-element.6), channel_id=1, source_target_pairs={{2,0},{4,2},{6,4},{8,6},{10,8},{12,10},{14,12},{3,1},{5,3},{7,5},{... | collective-permute-start | bytes 1474568 | tf_op jit(solution)/shard_map/ppermute | solution.py:17
where the time goes:
time: 430 us; the launch traced here: 426 us
  matrix products  267 us (62%)
  waiting for transfers between devices  89.9 us (21%)
  starting transfers between devices  50.9 us (12%)
  local copies, waits for them, and re-layouts  14.7 us (3%)
    dot_general x4, matrix products, blur(): jnp.einsum('zyx,xw->zyw', volume, table_x, precision=lax.Precision.HIGHEST)  101 us
    dot_general x4, matrix products, blur(): jnp.einsum('zyx,zw->wyx', along_y, table_z, precision=lax.Precision.HIGHEST)  83.9 us
    dot_general x4, matrix products, blur(): jnp.einsum('zyx,yw->zwx', widened, table_y, precision=lax.Precision.HIGHEST)  81.3 us
    ppermute x8, waiting for transfers between devices, padded(): lax.ppermute(tail, axis, [(i, (i + 1) % count) for i in range(ends)])  63.1 us
    ppermute x8, starting transfers between devices, padded(): lax.ppermute(head, axis, [((i + 1) % count, i) for i in range(ends)])  32.3 us
    ppermute x8, waiting for transfers between devices, padded(): lax.ppermute(head, axis, [((i + 1) % count, i) for i in range(ends)])  17.3 us
    ppermute x8, starting transfers between devices, padded(): lax.ppermute(tail, axis, [(i, (i + 1) % count) for i in range(ends)])  12.9 us
    all_to_all x1, waiting for transfers between devices, shards(): lax.all_to_all(view_b_own, 'gz', split_axis=2, concat_axis=0, tiled=True)  9.45 us
  transfers between devices with their start and end apart: 17, of which 11 were waited for; matrix products, arithmetic and copies ran while one was open for 2% of the time, Pallas kernels for 0%

commit v1 on v0

--- a/solution.py
+++ b/solution.py
@@ -1,7 +1,14 @@
+import functools
+
 import jax
 import jax.numpy as jnp
 from jax import lax
+from jax.experimental import pallas as pl
+from jax.experimental.pallas import tpu as pltpu
 from jax.sharding import PartitionSpec as P
+
+LANES = 128
+QUARTERS = 4
 
 
 def padded(cells, sides, width):
@@ -56,7 +63,315 @@
     return estimate
 
 
+def block_transpose(parts, width):
+    lane = lax.broadcasted_iota(jnp.int32, parts[0].shape, 1)
+    for step in (2, 1):
+        shift = step * width
+        low = lax.rem(lane // shift, 2) == 0
+        out = list(parts)
+        for first in range(QUARTERS):
+            if first & step:
+                continue
+            second = first + step
+            out[first] = jnp.where(low, parts[first], pltpu.roll(parts[second], shift, 1))
+            out[second] = jnp.where(low, pltpu.roll(parts[first], LANES - shift, 1), parts[second])
+        parts = out
+    return parts
+
+
+def split(values):
+    high = values.astype(jnp.bfloat16)
+    return high, (values - high.astype(jnp.float32)).astype(jnp.bfloat16)
+
+
+def dot(a, b):
+    return jnp.dot(a, b, preferred_element_type=jnp.float32)
+
+
+def deconvolve(
+    va_ref, vb_ref, sa_ref, sb_ref, out_ref,
+    send_a, recv_a, recv_b, view_a, view_b, estimate, blurred, work, halo_left, halo_right,
+    send_e, recv_e, tz_high, tz_low, ty_high, ty_low,
+    a_send_sem, a_recv_sem, b_sem, h_send_sem, h_recv_sem, e_send_sem, e_recv_sem,
+):
+    f32 = jnp.float32
+    groups = lax.axis_size("gz")
+    devices = 2 * groups
+    block = lax.axis_index("blocks")
+    gz, gy = lax.axis_index("gz"), lax.axis_index("gy")
+    me = 2 * gz + gy
+    slab = 2 * (groups - 1 - gz) + gy
+    deep, tall, _ = va_ref.shape
+    wide, full_y, full_z = view_a.shape
+    taps = sa_ref.shape[1]
+    radius = (taps - 1) // 2
+    rows_y = tall // QUARTERS
+    spreads = (sa_ref, sb_ref)
+
+    def slab_of(device):
+        return 2 * (groups - 1 - device // 2) + lax.rem(device, 2)
+
+    def at(device):
+        return (block, device // 2, lax.rem(device, 2))
+
+    barrier = pltpu.get_barrier_semaphore()
+    for hop in range(1, devices):
+        pl.semaphore_signal(
+            barrier, inc=1, device_id=at(lax.rem(me + hop, devices)), device_id_type=pl.DeviceIdType.MESH
+        )
+
+    for y in range(rows_y):
+        for column in range(va_ref.shape[2] // LANES):
+            parts = [
+                va_ref[:, q * rows_y + y, column * LANES:(column + 1) * LANES] for q in range(QUARTERS)
+            ]
+            for k, part in enumerate(block_transpose(parts, wide)):
+                send_a[QUARTERS * column + k, y] = part
+
+    pl.semaphore_wait(barrier, devices - 1)
+
+    half = pltpu.make_async_remote_copy(
+        src_ref=vb_ref.at[pl.ds(wide * gy, wide)],
+        dst_ref=recv_b,
+        send_sem=b_sem.at[0],
+        recv_sem=b_sem.at[1],
+        device_id=(block, gz, 1 - gy),
+        device_id_type=pl.DeviceIdType.MESH,
+    )
+    half.start()
+    copies_a = []
+    for hop in range(1, devices):
+        target = lax.rem(me + hop, devices)
+        copy = pltpu.make_async_remote_copy(
+            src_ref=send_a.at[slab_of(target)],
+            dst_ref=recv_a.at[gy, :, pl.ds(pl.multiple_of(gz * deep, 8), deep)],
+            send_sem=a_send_sem.at[hop],
+            recv_sem=a_recv_sem.at[hop],
+            device_id=at(target),
+            device_id_type=pl.DeviceIdType.MESH,
+        )
+        copy.start()
+        copies_a.append(copy)
+    recv_a[gy, :, pl.ds(pl.multiple_of(gz * deep, 8), deep)] = send_a[slab]
+
+    row = lax.broadcasted_iota(jnp.int32, (full_z, LANES), 0)
+    col = lax.broadcasted_iota(jnp.int32, (full_z, LANES), 1)
+    for which, spread in enumerate(spreads):
+        total = f32(1.0)
+        for axis in range(3):
+            line = spread[axis, 0]
+            for tap in range(1, taps):
+                line = line + spread[axis, tap]
+            total = total * line
+        for flipped in range(2):
+            index = 2 * which + flipped
+            sign = -1 if flipped else 1
+            offset = sign * (row - col) + radius
+            table = jnp.zeros((full_z, LANES), f32)
+            for tap in range(taps):
+                table = jnp.where(offset == tap, spread[0, tap], table)
+            table = table / jnp.full((full_z, LANES), total, f32)
+            tz_high[index], tz_low[index] = split(table)
+            offset = jnp.where(row // full_y == col // full_y, sign * (col - row) + radius, -1)
+            table = jnp.zeros((LANES, LANES), f32)
+            for tap in range(taps):
+                table = jnp.where(offset == tap, spread[1, tap], table)
+            ty_high[index], ty_low[index] = split(table)
+
+    mine, other = pl.multiple_of(gy * tall, 8), pl.multiple_of((1 - gy) * tall, 8)
+    for x in range(wide):
+        view_b[x, pl.ds(mine, tall)] = vb_ref[2 * wide - 1 - wide * gy - x]
+    half.wait()
+    for x in range(wide):
+        view_b[x, pl.ds(other, tall)] = recv_b[wide - 1 - x]
+
+    for copy in copies_a:
+        copy.wait_recv()
+    for side in range(2):
+        for y in range(rows_y):
+            turned = recv_a[side, y].T
+            for q in range(QUARTERS):
+                view_a[:, side * tall + q * rows_y + y, :] = turned[q * wide:(q + 1) * wide]
+
+    planes = LANES // full_y
+    chunks = wide // planes
+
+    def along_zy(values, index):
+        high, low = split(values.reshape(LANES, full_z))
+        zh = tz_high[index]
+        done = dot(high, zh) + (dot(low, zh) + dot(high, tz_low[index]))
+        high, low = split(done)
+        yh = ty_high[index]
+        done = dot(yh, high) + (dot(yh, low) + dot(ty_low[index], high))
+        return done.reshape(planes, full_y, full_z)
+
+    has_left, has_right = slab > 0, slab < devices - 1
+
+    def device_of(place):
+        return (block, groups - 1 - place // 2, lax.rem(place, 2))
+
+    left, right = device_of(jnp.maximum(slab - 1, 0)), device_of(jnp.minimum(slab + 1, devices - 1))
+
+    def x_taps(turn, spread, flipped, source, first, outputs, fresh):
+        count = source.shape[0]
+
+        def body(part, carry):
+            ys = pl.ds(pl.multiple_of(part * 8, 8), 8)
+            weights = [spread[2, taps - 1 - tap if flipped else tap] for tap in range(taps)]
+            for x in outputs:
+                total = None if fresh else blurred[x, ys]
+                for tap in range(taps):
+                    place = x + tap - radius - first
+                    if 0 <= place < count:
+                        term = weights[tap] * source[place, ys]
+                        total = term if total is None else total + term
+                blurred[x, ys] = total
+            return carry
+
+        lax.fori_loop(0, full_y // 8, body, 0)
+
+    def blur(turn, which, flipped, values):
+        index = 2 * which + flipped
+        spread = spreads[which]
+        held = work.at[turn]
+        to_left = pltpu.make_async_remote_copy(
+            src_ref=held.at[pl.ds(0, radius)],
+            dst_ref=halo_right.at[turn],
+            send_sem=h_send_sem.at[turn, 0],
+            recv_sem=h_recv_sem.at[turn, 0],
+            device_id=left,
+            device_id_type=pl.DeviceIdType.MESH,
+        )
+        to_right = pltpu.make_async_remote_copy(
+            src_ref=held.at[pl.ds(wide - radius, radius)],
+            dst_ref=halo_left.at[turn],
+            send_sem=h_send_sem.at[turn, 1],
+            recv_sem=h_recv_sem.at[turn, 1],
+            device_id=right,
+            device_id_type=pl.DeviceIdType.MESH,
+        )
+        for chunk in range(chunks):
+            span = pl.ds(chunk * planes, planes)
+            held[span] = along_zy(values(span), index)
+            if chunk == (radius - 1) // planes:
+                pl.when(has_left)(to_left.start)
+        pl.when(has_right)(to_right.start)
+        x_taps(turn, spread, flipped, held, 0, range(wide), True)
+
+        @pl.when(has_left)
+        def _():
+            to_right.wait_recv()
+            x_taps(turn, spread, flipped, halo_left.at[turn], -radius, range(radius), False)
+
+        @pl.when(has_right)
+        def _():
+            to_left.wait_recv()
+            x_taps(turn, spread, flipped, halo_right.at[turn], wide, range(wide - radius, wide), False)
+
+        pl.when(has_left)(to_left.wait_send)
+        pl.when(has_right)(to_right.wait_send)
+
+    def start_values(span):
+        estimate[span] = 0.5 * (view_a[span] + view_b[span])
+        return estimate[span]
+
+    def next_values(span):
+        estimate[span] = estimate[span] * blurred[span]
+        return estimate[span]
+
+    blur(0, 0, 0, start_values)
+    blur(1, 0, 1, lambda span: view_a[span] / blurred[span])
+    blur(2, 1, 0, next_values)
+    blur(3, 1, 1, lambda span: view_b[span] / blurred[span])
+    for chunk in range(chunks):
+        next_values(pl.ds(chunk * planes, planes))
+
+    for side in range(2):
+        for y in range(rows_y):
+            lines = [estimate[:, side * tall + q * rows_y + y, :] for q in range(QUARTERS)]
+            send_e[side, y] = jnp.concatenate(lines, axis=0).T
+    copies_e = []
+    for hop in range(1, devices):
+        target = lax.rem(me + hop, devices)
+        copy = pltpu.make_async_remote_copy(
+            src_ref=send_e.at[lax.rem(target, 2), :, pl.ds(pl.multiple_of(target // 2 * deep, 8), deep)],
+            dst_ref=recv_e.at[slab],
+            send_sem=e_send_sem.at[hop],
+            recv_sem=e_recv_sem.at[hop],
+            device_id=at(target),
+            device_id_type=pl.DeviceIdType.MESH,
+        )
+        copy.start()
+        copies_e.append(copy)
+    recv_e[slab] = send_e[gy, :, pl.ds(pl.multiple_of(gz * deep, 8), deep)]
+    for copy in copies_e:
+        copy.wait_recv()
+    for y in range(rows_y):
+        for column in range(va_ref.shape[2] // LANES):
+            parts = [recv_e[QUARTERS * column + k, y] for k in range(QUARTERS)]
+            for q, part in enumerate(block_transpose(parts, wide)):
+                out_ref[q * rows_y + y, :, column * LANES:(column + 1) * LANES] = part
+    for copy in copies_a + copies_e:
+        copy.wait_send()
+
+
+def slab_shards(view_a, view_b_own, spread_a, spread_b):
+    groups = lax.axis_size("gz")
+    deep, tall, long_x = view_a.shape
+    devices = 2 * groups
+    wide = long_x // devices
+    full_y, full_z = 2 * tall, view_b_own.shape[2]
+    taps = spread_a.shape[1]
+    radius = (taps - 1) // 2
+    f32, bf16 = jnp.float32, jnp.bfloat16
+    volume = pltpu.VMEM((wide, full_y, full_z), f32)
+    rows_y = tall // QUARTERS
+    turned = pl.pallas_call(
+        deconvolve,
+        out_shape=jax.ShapeDtypeStruct((tall, deep, long_x), f32),
+        in_specs=[pl.BlockSpec(memory_space=pltpu.VMEM)] * 2 + [pl.BlockSpec(memory_space=pltpu.SMEM)] * 2,
+        out_specs=pl.BlockSpec(memory_space=pltpu.VMEM),
+        scratch_shapes=[
+            pltpu.VMEM((devices, rows_y, deep, LANES), f32),
+            pltpu.VMEM((2, rows_y, full_z, LANES), f32),
+            pltpu.VMEM((wide, tall, full_z), f32),
+            volume, volume, volume, volume,
+            pltpu.VMEM((4, wide, full_y, full_z), f32),
+            pltpu.VMEM((4, radius, full_y, full_z), f32),
+            pltpu.VMEM((4, radius, full_y, full_z), f32),
+            pltpu.VMEM((2, rows_y, full_z, LANES), f32),
+            pltpu.VMEM((devices, rows_y, deep, LANES), f32),
+            pltpu.VMEM((4, full_z, full_z), bf16), pltpu.VMEM((4, full_z, full_z), bf16),
+            pltpu.VMEM((4, LANES, LANES), bf16), pltpu.VMEM((4, LANES, LANES), bf16),
+            pltpu.SemaphoreType.DMA((devices,)), pltpu.SemaphoreType.DMA((devices,)),
+            pltpu.SemaphoreType.DMA((2,)),
+            pltpu.SemaphoreType.DMA((4, 2)), pltpu.SemaphoreType.DMA((4, 2)),
+            pltpu.SemaphoreType.DMA((devices,)), pltpu.SemaphoreType.DMA((devices,)),
+        ],
+        compiler_params=pltpu.CompilerParams(
+            collective_id=0, has_side_effects=True, vmem_limit_bytes=48 * 1024 * 1024
+        ),
+    )(view_a, view_b_own, spread_a, spread_b)
+    return jnp.transpose(turned, (1, 0, 2))
+
+
+def fits_slabs(mesh, view_a, view_b_own, spread_a):
+    groups, sides = mesh.shape["gz"], mesh.shape["gy"]
+    deep = view_a[0] // (mesh.shape["blocks"] * groups)
+    tall, wide = view_a[1] // sides, view_a[2] // (2 * groups)
+    return (
+        sides == 2 and wide * QUARTERS == LANES and view_b_own[2] == LANES and 4 * view_a[1] == LANES
+        and tall % (8 * sides) == 0 and deep % 8 == 0 and spread_a[1] % 2 == 1 and spread_a[1] // 2 <= wide // 2
+    )
+
+
 def solution(mesh):
     in_specs = (P(("blocks", "gz"), "gy", None), P(("blocks", "gz"), "gy", None), P(), P())
     out_specs = P(("blocks", "gz"), "gy", None)
-    return jax.shard_map(shards, mesh=mesh, in_specs=in_specs, out_specs=out_specs, check_vma=False)
+
+    def run(view_a, view_b_own, spread_a, spread_b):
+        plan = slab_shards if fits_slabs(mesh, view_a.shape, view_b_own.shape, spread_a.shape) else shards
+        split_plan = jax.shard_map(plan, mesh=mesh, in_specs=in_specs, out_specs=out_specs, check_vma=False)
+        return split_plan(view_a, view_b_own, spread_a, spread_b)
+
+    return run

time: 430 us -> 64 us (0.15)
  the two profiles are of different devices: /device:TPU:9 before, /device:TPU:1 now
where the time goes in v1:
time: 64 us; the launch traced here: 63.7 us
  Pallas kernels  59.2 us (92%)
  local copies, waits for them, and re-layouts  4.55 us (7%)
    pallas_call x1, Pallas kernels, slab_shards(): pl.pallas_call(deconvolve, out_shape=jax.ShapeDtypeStruct((tall, deep, lo...  59.2 us
    unnamed x8, local copies, waits for them, and re-layouts  3.44 us

profile of v1, /device:TPU:1, one launch (start us, length us, event | category | flops | bytes accessed | tf_op | source)
XLA Modules:
  0.0 63.7 jit_solution(18257440986211612222)
XLA Ops:
  0.0 0.0 copy-start
  0.0 1.0 %copy-done = f32[16,16,512]{2,1,0:T(8,128)S(1)} copy-done((f32[16,16,512]{2,1,0:T(8,128)S(1)}, f32[16,16,512]{2,1,0:T(8,128)}, u32[]{:S(2)}) %copy-start) | copy-done | bytes 524312
  1.0 0.0 copy-start.1
  1.0 1.0 %copy-done.1 = f32[64,16,128]{2,1,0:T(8,128)S(1)} copy-done((f32[64,16,128]{2,1,0:T(8,128)S(1)}, f32[64,16,128]{2,1,0:T(8,128)}, u32[]{:S(2)}) %copy-start.1) | copy-done | bytes 524312
  2.1 0.0 copy-start.2
  2.1 0.7 %copy-done.2 = f32[3,31]{1,0:T(4,128)S(1)} copy-done((f32[3,31]{1,0:T(4,128)S(1)}, f32[3,31]{1,0:T(4,128)}, u32[]{:S(2)}) %copy-start.2) | copy-done | bytes 396
  2.8 0.0 copy-start.3
  2.8 0.7 %copy-done.3 = f32[3,31]{1,0:T(4,128)S(1)} copy-done((f32[3,31]{1,0:T(4,128)S(1)}, f32[3,31]{1,0:T(4,128)}, u32[]{:S(2)}) %copy-start.3) | copy-done | bytes 396
  3.4 59.2 %shard_map.46 = f32[16,16,512]{2,1,0:T(8,128)S(1)} custom-call(f32[16,16,512]{2,1,0:T(8,128)S(1)} %copy-done, f32[64,16,128]{2,1,0:T(8,128)S(1)} %copy-done.1, f32[3,31]{1,0:T(4,128)S(1)} %copy-done.2, f32[3,31]{1,0:T(4,128)S(1)} %copy-done.3), custom_call_target="tpu_custom_call" | custom-call | tf_op jit(solution)/shard_map/pallas_call | solution.py:329
  62.6 1.1 %copy.5 = f32[16,16,512]{2,1,0:T(8,128)} copy(f32[16,16,512]{2,0,1:T(8,128)S(1)} %bitcast.1) | data formatting | bytes 1048576 | tf_op jit(solution)/shard_map/transpose | solution.py:355
Async XLA Ops:
  0.0 1.0 %copy-start = (f32[16,16,512]{2,1,0:T(8,128)S(1)}, f32[16,16,512]{2,1,0:T(8,128)}, u32[]{:S(2)}) copy-start(f32[16,16,512]{2,1,0:T(8,128)} %va_ref.1) | copy-start | bytes 1572868
  1.0 1.0 %copy-start.1 = (f32[64,16,128]{2,1,0:T(8,128)S(1)}, f32[64,16,128]{2,1,0:T(8,128)}, u32[]{:S(2)}) copy-start(f32[64,16,128]{2,1,0:T(8,128)} %vb_ref.1) | copy-start | bytes 1572868
  2.1 0.7 %copy-start.2 = (f32[3,31]{1,0:T(4,128)S(1)}, f32[3,31]{1,0:T(4,128)}, u32[]{:S(2)}) copy-start(f32[3,31]{1,0:T(4,128)} %sa_ref.1) | copy-start | bytes 1120
  2.8 0.7 %copy-start.3 = (f32[3,31]{1,0:T(4,128)S(1)}, f32[3,31]{1,0:T(4,128)}, u32[]{:S(2)}) copy-start(f32[3,31]{1,0:T(4,128)} %sb_ref.1) | copy-start | bytes 1120
